TPU v7x, 32 devices: a whole 2x2x4 slice. The times are simulated.
32 devices in a mesh: dp: 2 (over x), kv: 4 (over z), tp: 4 (over y, core).
Axes of the slice: x: 2, y: 2, z: 4, core: 2. Of those that a mesh axis runs over, the one named last changes fastest.
Arguments:
- x: bfloat16 [16, 5120], P('dp'), parts along dimension 0
- ks_cache: bfloat16 [16, 8, 1024, 128], P('dp', 'tp', 'kv'), parts along dimension 0
- vs_cache: bfloat16 [16, 8, 1024, 128], P('dp', 'tp', 'kv'), parts along dimension 0
- seq_len: int32 [16], P('dp'), parts along dimension 0
- kx_cache: bfloat16 [16, 8, 6404, 128], P('dp', 'tp', 'kv'), parts along dimension 0
- vx_cache: bfloat16 [16, 8, 6404, 128], P('dp', 'tp', 'kv'), parts along dimension 0
- tile_vis: int32 [16, 4], P('dp'), parts along dimension 0
- attn_norm: bfloat16 [5120], replicated
- wq_self: bfloat16 [5120, 5120], P(None, 'tp')
- wk_self: bfloat16 [5120, 1024], P(None, 'tp')
- wv_self: bfloat16 [5120, 1024], P(None, 'tp')
- wo_self: bfloat16 [5120, 5120], P('tp')
- mlp_norm: bfloat16 [5120], replicated
- wg_self: bfloat16 [5120, 13824], P(None, 'tp')
- wu_self: bfloat16 [5120, 13824], P(None, 'tp')
- wd_self: bfloat16 [13824, 5120], P('tp')
- xattn_norm: bfloat16 [5120], replicated
- wq_cross: bfloat16 [5120, 5120], P(None, 'tp')
- q_norm: bfloat16 [128], replicated
- wo_cross: bfloat16 [5120, 5120], P('tp')
- cross_gates: float32 [2], replicated
- xmlp_norm: bfloat16 [5120], replicated
- wg_cross: bfloat16 [5120, 13824], P(None, 'tp')
- wu_cross: bfloat16 [5120, 13824], P(None, 'tp')
- wd_cross: bfloat16 [13824, 5120], P('tp')
Outputs:
- output 1: bfloat16 [16, 5120], P('dp'), parts along dimension 0
- output 2: bfloat16 [16, 8, 128], P('dp', 'tp'), parts along dimension 0
- output 3: bfloat16 [16, 8, 128], P('dp', 'tp'), parts along dimension 0
There are 2 independent parts. A program takes and returns all parts, laid end to end along the dimension named above; an argument that names none is the same for every part.
All inputs are finite; a program needn't handle non-finite values.
Results may differ from a plain program's by a relative error of at most 0.0130243.
Values sent between devices are 32-bit elements.
A program may use at most 1.25 GiB of HBM per device.

v0:
```python
import math
import jax
import jax.numpy as jnp
from jax import lax
from jax.sharding import PartitionSpec as P

NORM_EPS = 1e-5
ROPE_THETA = 500000.0
MASK_VALUE = -1e30


def rope_freqs(head_dim):
    freq_list = []
    for index in range(head_dim // 2):
        base_freq = 1.0 / (ROPE_THETA ** (2.0 * index / head_dim))
        wave_len = 2.0 * math.pi / base_freq
        if wave_len < 2048.0:
            freq_list.append(base_freq)
        elif wave_len > 8192.0:
            freq_list.append(base_freq / 8.0)
        else:
            smooth = (8192.0 / wave_len - 1.0) / 3.0
            freq_list.append((1.0 - smooth) * base_freq / 8.0 + smooth * base_freq)
    return jnp.array(freq_list, dtype=jnp.float32)


def rms_norm(hidden, gain):
    return hidden * lax.rsqrt(jnp.mean(hidden * hidden, axis=-1, keepdims=True) + NORM_EPS) * gain.astype(jnp.float32)


def apply_rope(tensor, cos_t, sin_t):
    half = tensor.shape[-1] // 2
    first = tensor[..., :half]
    second = tensor[..., half:]
    return jnp.concatenate([first * cos_t - second * sin_t, second * cos_t + first * sin_t], axis=-1)


def swiglu_part(h_norm, w_gate, w_up, w_down):
    gate = jnp.dot(h_norm, w_gate, preferred_element_type=jnp.float32)
    upper = jnp.dot(h_norm, w_up, preferred_element_type=jnp.float32)
    hidden_act = (jax.nn.silu(gate) * upper).astype(jnp.bfloat16)
    return jnp.dot(hidden_act, w_down, preferred_element_type=jnp.float32)


def self_partial(query, keys, values, visible, key_new, val_new, owner):
    score_scale = query.shape[-1] ** -0.5
    mask = visible[:, None, None, :]
    owner_mask = owner[:, None, None]
    scores = jnp.einsum('bkgd,bktd->bkgt', query, keys, preferred_element_type=jnp.float32) * score_scale
    scores = jnp.where(mask, scores, MASK_VALUE)
    new_score = jnp.einsum('clhe,cle->clh', query, key_new, preferred_element_type=jnp.float32) * score_scale
    new_score = jnp.where(owner_mask, new_score, MASK_VALUE)
    top = jnp.maximum(jnp.max(scores, axis=-1), new_score)
    probs = jnp.where(mask, jnp.exp(scores - top[..., None]), 0.0)
    new_prob = jnp.where(owner_mask, jnp.exp(new_score - top), 0.0)
    total = jnp.sum(probs, axis=-1) + new_prob
    out = jnp.einsum('bkgt,bktd->bkgd', probs.astype(jnp.bfloat16), values, preferred_element_type=jnp.float32) + new_prob[..., None] * val_new[:, :, None, :].astype(jnp.float32)
    return out, top, total


def cross_partial(query, keys, values, visible):
    mask = visible[:, None, None, :, None]
    scores = jnp.einsum('bkgd,bkstd->bkgst', query, keys, preferred_element_type=jnp.float32) * query.shape[-1] ** -0.5
    scores = jnp.where(mask, scores, MASK_VALUE)
    top = jnp.max(scores, axis=(3, 4))
    probs = jnp.where(mask, jnp.exp(scores - top[..., None, None]), 0.0)
    total = jnp.sum(probs, axis=(3, 4))
    out = jnp.einsum('bkgst,bkstd->bkgd', probs.astype(jnp.bfloat16), values, preferred_element_type=jnp.float32)
    return out, top, total


def combine_partials(out, top, total):
    head_dim = out.shape[-1]
    packed = jnp.concatenate([out, top[..., None], total[..., None]], axis=-1)
    gathered = lax.all_gather(packed, 'kv', axis=0)
    tops = gathered[..., head_dim]
    best = jnp.max(tops, axis=0)
    weight = jnp.exp(tops - best[None])
    weight_sum = jnp.sum(gathered[..., head_dim + 1] * weight, axis=0)
    combined = jnp.sum(gathered[..., :head_dim] * weight[..., None], axis=0)
    return (combined / jnp.where(weight_sum > 0, weight_sum, 1.0)[..., None]).astype(jnp.bfloat16)


def solution(mesh):
    kv_size = mesh.shape['kv']
    rows_spec = P('dp', None)
    cache_spec = P('dp', 'tp', 'kv', None)
    new_spec = P('dp', 'tp', None)
    col_spec = P(None, 'tp')
    row_spec = P('tp', None)
    vec_spec = P(None)
    in_specs = (rows_spec, cache_spec, cache_spec, P('dp'), cache_spec, cache_spec, rows_spec,
                vec_spec, col_spec, col_spec, col_spec, row_spec, vec_spec, col_spec, col_spec, row_spec,
                vec_spec, col_spec, vec_spec, row_spec, vec_spec, vec_spec, col_spec, col_spec, row_spec)
    out_specs = (rows_spec, new_spec, new_spec)

    def device_step(x, ks_cache, vs_cache, seq_len, kx_cache, vx_cache, tile_vis, attn_norm, wq_self, wk_self, wv_self, wo_self, mlp_norm, wg_self, wu_self, wd_self, xattn_norm, wq_cross, q_norm, wo_cross, cross_gates, xmlp_norm, wg_cross, wu_cross, wd_cross):
        batch = x.shape[0]
        kv_local = ks_cache.shape[1]
        shard_len = ks_cache.shape[2]
        head_dim = ks_cache.shape[3]
        heads_local = wq_self.shape[1] // head_dim
        group = heads_local // kv_local
        tiles_local = tile_vis.shape[1] // kv_size
        tile_tok = kx_cache.shape[2] // tiles_local
        kv_index = lax.axis_index('kv')
        angles = seq_len.astype(jnp.float32)[:, None] * rope_freqs(head_dim)[None, :]
        cos_t = jnp.cos(angles)[:, None, :]
        sin_t = jnp.sin(angles)[:, None, :]
        x_float = x.astype(jnp.float32)
        x_norm = rms_norm(x_float, attn_norm).astype(jnp.bfloat16)
        query = apply_rope(jnp.dot(x_norm, wq_self, preferred_element_type=jnp.float32).reshape(batch, heads_local, head_dim), cos_t, sin_t)
        query = query.astype(jnp.bfloat16).reshape(batch, kv_local, group, head_dim)
        key_new = apply_rope(jnp.dot(x_norm, wk_self, preferred_element_type=jnp.float32).reshape(batch, kv_local, head_dim), cos_t, sin_t).astype(jnp.bfloat16)
        val_new = jnp.dot(x_norm, wv_self, preferred_element_type=jnp.float32).astype(jnp.bfloat16).reshape(batch, kv_local, head_dim)
        slot_ids = kv_index * shard_len + jnp.arange(shard_len)
        visible_self = slot_ids[None, :] < seq_len[:, None]
        owner = (seq_len // shard_len) == kv_index
        out, top, total = self_partial(query, ks_cache, vs_cache, visible_self, key_new, val_new, owner)
        attn_self = combine_partials(out, top, total).reshape(batch, heads_local * head_dim)
        proj_self = lax.psum(jnp.dot(attn_self, wo_self, preferred_element_type=jnp.float32), 'tp')
        h_one = (x_float + proj_self).astype(jnp.bfloat16)
        h_one_f = h_one.astype(jnp.float32)
        mlp_self = swiglu_part(rms_norm(h_one_f, mlp_norm).astype(jnp.bfloat16), wg_self, wu_self, wd_self)
        h_two = (h_one_f + lax.psum(mlp_self, 'tp')).astype(jnp.bfloat16)
        h_two_f = h_two.astype(jnp.float32)
        cx_norm = rms_norm(h_two_f, xattn_norm).astype(jnp.bfloat16)
        query_x = jnp.dot(cx_norm, wq_cross, preferred_element_type=jnp.float32).reshape(batch, heads_local, head_dim)
        query_x = rms_norm(query_x, q_norm).astype(jnp.bfloat16).reshape(batch, kv_local, group, head_dim)
        tile_on = tile_vis != 0
        tiles_here = lax.dynamic_slice_in_dim(tile_on, kv_index * tiles_local, tiles_local, axis=1)
        kx_tiles = kx_cache.reshape(batch, kv_local, tiles_local, tile_tok, head_dim)
        vx_tiles = vx_cache.reshape(batch, kv_local, tiles_local, tile_tok, head_dim)
        out_x, top_x, total_x = cross_partial(query_x, kx_tiles, vx_tiles, tiles_here)
        attn_cross = combine_partials(out_x, top_x, total_x).reshape(batch, heads_local * head_dim)
        row_on = jnp.any(tile_on, axis=1).astype(jnp.float32)[:, None]
        gates = jnp.tanh(cross_gates)
        proj_cross = lax.psum(jnp.dot(attn_cross, wo_cross, preferred_element_type=jnp.float32), 'tp')
        h_three = (h_two_f + gates[0] * row_on * proj_cross).astype(jnp.bfloat16)
        h_three_f = h_three.astype(jnp.float32)
        mlp_cross = swiglu_part(rms_norm(h_three_f, xmlp_norm).astype(jnp.bfloat16), wg_cross, wu_cross, wd_cross)
        h_four = (h_three_f + gates[1] * row_on * lax.psum(mlp_cross, 'tp')).astype(jnp.bfloat16)
        return h_four, key_new, val_new

    return jax.shard_map(device_step, mesh=mesh, in_specs=in_specs, out_specs=out_specs, check_vma=False)
```

profile of v0, /device:TPU:0, one launch (start us, length us, event | category | flops | bytes accessed | tf_op | source)
XLA Modules:
  0.0 305.4 jit_solution(3351519918738012407)
XLA Ops:
  7.2 0.0 all-reduce.5.cloned.1.call-start
  7.3 0.9 convert_element_type.103
  8.1 1.0 fusion.22
  9.2 1.4 convolution_bitcast_fusion.1
  10.6 0.1 fusion.94
  10.6 0.8 convert_element_type.105
  11.4 6.6 %convolution_bitcast_fusion = f32[8,10,128]{2,0,1:T(8,128)S(1)} fusion(bf16[5120,1280]{1,0:T(8,128)(2,1)} %param.34, bf16[8,5120]{1,0:T(8,128)(2,1)} %param.26, f32[5120]{0:T(1024)S(1)} %convert_element_type.103, f32[8]{0:T(128)S(1)} %add_rsqrt_fusion.4), kind=kOutput, calls=%fused_computation.15 | convolution fusion | flops 105021440 | bytes 13250592 | tf_op jit(solution)/shard_map/dot_general | solution.py:112
  18.0 0.1 multiply_cosine_fusion
  18.2 0.1 subtract_convert_fusion
  18.3 0.1 broadcast_compare_fusion
  18.4 0.1 fusion.116
  18.5 0.2 fusion.77
  18.7 1.7 fusion.96
  20.5 0.1 fusion.86
  20.6 0.2 fusion.50
  20.8 0.1 add_bitcast_fusion
  20.9 0.5 fusion.15
  21.4 0.2 copy.165
  21.6 0.2 copy.164
  21.8 1.5 convolution_add_fusion
  23.3 0.1 pad_maximum_fusion
  23.5 15.9 %all-gather = f32[32,2,5,130]{3,1,2,0:T(2,128)S(1)} all-gather(f32[8,2,5,130]{3,1,2,0:T(2,128)S(1)} %copy.166), channel_id=2, replica_groups=mesh['dp'=2,'kv'=4,'tp'=4] {'kv'}, dimensions={0}, use_global_device_ids=true | all-gather | bytes 208000 | tf_op jit(solution)/shard_map/all_gather | solution.py:75
  39.4 0.1 slice_reduce_fusion.5
  39.5 0.3 slice_reduce_fusion.4
  39.9 0.1 copy.169
  40.0 0.1 fusion.39
  40.1 0.1 fusion.58
  40.2 7.2 %fusion.98 = f32[8,5120]{1,0:T(8,128)} fusion(bf16[8,1280]{1,0:T(8,128)(2,1)S(1)} %convert_element_type.110, bf16[1280,5120]{1,0:T(8,128)(2,1)} %param.37), kind=kOutput, calls=%fused_computation.147 | convolution fusion | flops 104857600 | bytes 13291520 | tf_op jit(solution)/shard_map/dot_general | solution.py:121
  47.5 0.0 all-reduce.7.cloned.1.call-start
  47.6 0.6 fusion.95
  48.2 33.0 %all-reduce.5.cloned.1.call-done = f32[8,5120]{1,0:T(8,128)} async-done(((f32[8,5120]{1,0:T(8,128)}), f32[8,5120]{1,0:T(8,128)}) %all-reduce.5.cloned.1.call-update) | async-done | bytes 163856 | tf_op jit(solution)/shard_map/psum | solution.py:121
  81.2 1.1 fusion.26
  82.3 13.5 %fusion.75 = f32[8,3456]{1,0:T(8,128)S(1)} fusion(bf16[5120,3456]{1,0:T(8,128)(2,1)} %param.39, bf16[8,5120]{1,0:T(8,128)(2,1)S(1)} %get-tuple-element.34, f32[5120]{0:T(1024)S(1)} %convert_element_type.113, f32[8]{0:T(128)S(1)} %add_rsqrt_fusion.3), kind=kOutput, calls=%fused_computation.108 | convolution fusion | flops 283279360 | bytes 35602464 | tf_op jit(solution)/shard_map/dot_general | solution.py:39
  95.8 25.3 %fusion.7 = f32[8,5120]{1,0:T(8,128)} fusion(bf16[3456,5120]{1,0:T(8,128)(2,1)} %param.41, bf16[5120,3456]{1,0:T(8,128)(2,1)} %param.40, f32[8,3456]{1,0:T(8,128)S(1)} %fusion.75, bf16[8,5120]{1,0:T(8,128)(2,1)S(1)} %get-tuple-element.34, f32[5120]{0:T(1024)S(1)} %convert_element_type.113, f32[8]{0:T(128)S(1)} %add_rsqrt_fusion.3), kind=kOutput, calls=%fused_computation.9 | convolution fusion | flops 566560768 | bytes 71155744 | tf_op jit(solution)/shard_map/dot_general | solution.py:42
  121.1 0.0 all-reduce.7.cloned.1.call-update
  121.1 0.2 all-reduce.9.cloned.1.call-start
  121.4 31.7 %all-reduce.7.cloned.1.call-done = f32[8,5120]{1,0:T(8,128)} async-done(((f32[8,5120]{1,0:T(8,128)}), f32[8,5120]{1,0:T(8,128)}) %all-reduce.7.cloned.1.call-update) | async-done | bytes 163856 | tf_op jit(solution)/shard_map/psum | solution.py:125
  153.1 1.1 fusion.30
  154.2 6.6 %bitcast_reduce_fusion = (f32[8,10]{0,1:T(8,128)S(1)}, f32[8,1280]{1,0:T(8,128)S(1)}) fusion(bf16[5120,1280]{1,0:T(8,128)(2,1)} %param.43, bf16[8,5120]{1,0:T(8,128)(2,1)S(1)} %get-tuple-element.32, f32[5120]{0:T(1024)S(1)} %convert_element_type.118, f32[8]{0:T(128)S(1)} %add_rsqrt_fusion.2), kind=kOutput, calls=%fused_computation.97 | convolution fusion | flops 105041840 | bytes 13250912 | tf_op jit(solution)/shard_map/dot_general | solution.py:128
  160.8 0.1 copy.171
  160.9 0.1 rsqrt.47
  161.0 4.9 %fusion.97 = (f32[8,2,5]{2,1,0:T(2,128)S(1)}, f32[8,2,5,1601]{3,2,1,0:T(8,128)S(1)}) fusion(bf16[8,2,1601,128]{3,1,2,0:T(2,128)(2,1)} %param.30, f32[8,2,5,128]{3,0,2,1:T(8,128)S(1)} %bitcast.52, f32[128]{0:T(128)S(1)} %convert_element_type.120, f32[8,2,5]{2,1,0:T(2,128)S(1)} %rsqrt.47, pred[8]{0:T(512)(128)(4,1)S(1)} %dynamic-slice_bitcast_fusion), kind=kOutput, calls=%fused_computation.146 | convolution fusion | flops 33203360 | bytes 7112136 | tf_op jit(solution)/shard_map/bkgd,bkstd->bkgst/dot_general | solution.py:63
  165.9 0.3 fusion.16
  166.2 4.0 %fusion = f32[8,2,5,128]{3,2,1,0:T(8,128)S(1)} fusion(bf16[8,2,1601,128]{3,1,2,0:T(2,128)(2,1)} %param.31, f32[8,2,5,1601]{3,2,1,0:T(8,128)S(1)} %get-tuple-element.54, f32[8,2,5]{2,1,0:T(2,128)S(1)} %get-tuple-element.53, pred[8]{0:T(512)(128)(4,1)S(1)} %dynamic-slice_bitcast_fusion), kind=kOutput, calls=%fused_computation | convolution fusion | flops 33172720 | bytes 7111304 | tf_op jit(solution)/shard_map/bkgst,bkstd->bkgd/dot_general | solution.py:68
  170.2 0.2 copy.178
  170.4 0.2 copy.177
  170.6 0.1 pad_maximum_fusion.1
  170.8 14.0 %all-gather.1 = f32[32,2,5,130]{3,1,2,0:T(2,128)S(1)} all-gather(f32[8,2,5,130]{3,1,2,0:T(2,128)S(1)} %copy.179), channel_id=3, replica_groups=mesh['dp'=2,'kv'=4,'tp'=4] {'kv'}, dimensions={0}, use_global_device_ids=true | all-gather | bytes 208000 | tf_op jit(solution)/shard_map/all_gather | solution.py:75
  184.8 0.1 slice_reduce_fusion.3
  184.9 0.3 slice_reduce_fusion.2
  185.3 0.1 copy.182
  185.4 0.1 fusion.38
  185.5 0.1 fusion.57
  185.7 7.2 %fusion.99 = f32[8,5120]{1,0:T(8,128)} fusion(bf16[8,1280]{1,0:T(8,128)(2,1)S(1)} %convert_element_type.124, bf16[1280,5120]{1,0:T(8,128)(2,1)} %param.45), kind=kOutput, calls=%fused_computation.148 | convolution fusion | flops 104857600 | bytes 13291520 | tf_op jit(solution)/shard_map/dot_general | solution.py:138
  192.9 0.3 all-reduce.11.cloned.1.call-start
  193.1 1.3 broadcast_select_fusion
  194.4 0.6 copy.184
  195.1 30.1 %all-reduce.9.cloned.1.call-done = f32[8,5120]{1,0:T(8,128)} async-done(((f32[8,5120]{1,0:T(8,128)}), f32[8,5120]{1,0:T(8,128)}) %all-reduce.9.cloned.1.call-update) | async-done | bytes 163856 | tf_op jit(solution)/shard_map/psum | solution.py:138
  225.2 1.1 fusion.34
  226.3 13.5 %fusion.71 = f32[8,3456]{1,0:T(8,128)S(1)} fusion(bf16[5120,3456]{1,0:T(8,128)(2,1)} %param.48, bf16[8,5120]{1,0:T(8,128)(2,1)S(1)} %get-tuple-element.28, f32[5120]{0:T(1024)S(1)} %convert_element_type.127, f32[8]{0:T(128)S(1)} %add_rsqrt_fusion.1), kind=kOutput, calls=%fused_computation.107 | convolution fusion | flops 283279360 | bytes 35602464 | tf_op jit(solution)/shard_map/dot_general | solution.py:39
  239.8 25.4 %fusion.6 = f32[8,5120]{1,0:T(8,128)} fusion(bf16[3456,5120]{1,0:T(8,128)(2,1)} %param.50, bf16[5120,3456]{1,0:T(8,128)(2,1)} %param.49, f32[8,3456]{1,0:T(8,128)S(1)} %fusion.71, bf16[8,5120]{1,0:T(8,128)(2,1)S(1)} %get-tuple-element.28, f32[5120]{0:T(1024)S(1)} %convert_element_type.127, f32[8]{0:T(128)S(1)} %add_rsqrt_fusion.1), kind=kOutput, calls=%fused_computation.8 | convolution fusion | flops 566560768 | bytes 71155744 | tf_op jit(solution)/shard_map/dot_general | solution.py:42
  265.2 0.7 pad_maximum_fusion.5
  265.9 31.3 %all-reduce.11.cloned.1.call-done = f32[8,5120]{1,0:T(8,128)} async-done(((f32[8,5120]{1,0:T(8,128)}), f32[8,5120]{1,0:T(8,128)}) %all-reduce.11.cloned.1.call-update) | async-done | bytes 163856 | tf_op jit(solution)/shard_map/psum | solution.py:142
  297.2 1.6 fusion.37
  (55 shorter events, 0.6 us)
Async XLA Ops:
  7.2 2.0 copy-start
  7.2 10.9 %copy-start.9 = (f32[64]{0:T(128)S(1)}, f32[64]{0:T(128)}, u32[]{:S(2)}) copy-start(f32[64]{0:T(128)} %constant.60.clone) | copy-start | bytes 772
  7.2 13.7 %copy-start.3 = (bf16[8,5120]{1,0:T(8,128)(2,1)S(1)}, bf16[8,5120]{1,0:T(8,128)(2,1)}, u32[]{:S(2)}) copy-start(bf16[8,5120]{1,0:T(8,128)(2,1)} %param.26) | copy-start | bytes 245764
  7.2 11.1 %copy-start.8 = (s32[8]{0:T(128)S(1)}, s32[8]{0:T(128)}, u32[]{:S(2)}) copy-start(s32[8]{0:T(128)} %param.29) | copy-start | bytes 100
  7.2 74.0 %all-reduce.5.cloned.1.call-start = ((), (), s32[]{:S(2)}) async-start(), calls=%async_computation | async-start | bytes 327680 | tf_op jit(solution)/shard_map/psum | solution.py:121
  10.6 10.3 %copy-start.2 = (bf16[5120,256]{1,0:T(8,128)(2,1)S(1)}, bf16[5120,256]{1,0:T(8,128)(2,1)}, u32[]{:S(2)}) copy-start(bf16[5120,256]{1,0:T(8,128)(2,1)} %param.36) | copy-start | bytes 7864324
  20.5 27.1 %copy-start.4 = (bf16[5120]{0:T(1024)(128)(2,1)S(1)}, bf16[5120]{0:T(1024)(128)(2,1)}, u32[]{:S(2)}) copy-start(bf16[5120]{0:T(1024)(128)(2,1)} %param.38) | copy-start | bytes 30724
  20.5 27.1 %copy-start.5 = (bf16[5120]{0:T(1024)(128)(2,1)S(1)}, bf16[5120]{0:T(1024)(128)(2,1)}, u32[]{:S(2)}) copy-start(bf16[5120]{0:T(1024)(128)(2,1)} %param.42) | copy-start | bytes 30724
  20.5 27.1 %copy-start.7 = (s32[8,4]{0,1:T(4,128)S(1)}, s32[8,4]{0,1:T(4,128)}, u32[]{:S(2)}) copy-start(s32[8,4]{0,1:T(4,128)} %param.32) | copy-start | bytes 388
  20.5 27.1 %copy-start.10 = (bf16[128]{0:T(256)(128)(2,1)S(1)}, bf16[128]{0:T(256)(128)(2,1)}, u32[]{:S(2)}) copy-start(bf16[128]{0:T(256)(128)(2,1)} %param.44) | copy-start | bytes 772
  20.5 27.1 %copy-start.11 = (f32[2]{0:T(128)S(1)}, f32[2]{0:T(128)}, u32[]{:S(2)}) copy-start(f32[2]{0:T(128)} %param.46) | copy-start | bytes 28
  47.5 105.7 %all-reduce.7.cloned.1.call-start = ((), (), s32[]{:S(2)}) async-start(), calls=%async_computation.1 | async-start | bytes 327680 | tf_op jit(solution)/shard_map/psum | solution.py:125
  121.1 104.0 %all-reduce.9.cloned.1.call-start = ((), (), s32[]{:S(2)}) async-start(), calls=%async_computation.2 | async-start | bytes 327680 | tf_op jit(solution)/shard_map/psum | solution.py:138
  166.2 28.8 %copy-start.6 = (bf16[5120]{0:T(1024)(128)(2,1)S(1)}, bf16[5120]{0:T(1024)(128)(2,1)}, u32[]{:S(2)}) copy-start(bf16[5120]{0:T(1024)(128)(2,1)} %param.47) | copy-start | bytes 30724
  192.9 104.4 %all-reduce.11.cloned.1.call-start = ((), (), s32[]{:S(2)}) async-start(), calls=%async_computation.3 | async-start | bytes 327680 | tf_op jit(solution)/shard_map/psum | solution.py:142
  239.8 59.1 %copy-start.1 = (bf16[5120,256]{1,0:T(8,128)(2,1)S(1)}, bf16[5120,256]{1,0:T(8,128)(2,1)}, u32[]{:S(2)}) copy-start(bf16[5120,256]{1,0:T(8,128)(2,1)} %param.35) | copy-start | bytes 7864324
Sparse Core Ops, SparseCore 0:
  47.6 33.5 all-reduce.4
  121.2 31.8 all-reduce.6
  193.0 32.1 all-reduce.8
  265.4 31.8 all-reduce.10
where the time goes:
time: 306 us; the launch traced here: 305 us
  waiting for transfers between devices  126 us (41%)
  matrix products  120 us (39%)
  blocking collectives  30 us (10%)
  between operations  14.1 us (5%)
  other arithmetic  12.2 us (4%)
    dot_general x2, matrix products, swiglu_part(): return jnp.dot(hidden_act, w_down, preferred_element_type=jnp.float32)  50.7 us
    psum x1, waiting for transfers between devices, device_step(): lax.psum(jnp.dot(attn_self, wo_self, preferred_element_type=jnp.float32),...  33 us
    psum x1, waiting for transfers between devices, device_step(): h_two = (h_one_f + lax.psum(mlp_self, 'tp')).astype(jnp.bfloat16)  31.7 us
    psum x1, waiting for transfers between devices, device_step(): lax.psum(mlp_cross, 'tp')  31.3 us
    psum x1, waiting for transfers between devices, device_step(): lax.psum(jnp.dot(attn_cross, wo_cross, preferred_element_type=jnp.float32...  30.1 us
    all_gather x2, blocking collectives, combine_partials(): gathered = lax.all_gather(packed, 'kv', axis=0)  30 us
    dot_general x2, matrix products, swiglu_part(): gate = jnp.dot(h_norm, w_gate, preferred_element_type=jnp.float32)  27.1 us
    dot_general x1, matrix products, device_step(): jnp.dot(attn_self, wo_self, preferred_element_type=jnp.float32)  7.19 us
  transfers between devices with their start and end apart: 4, of which 4 were waited for; matrix products, arithmetic and copies ran while one was open for 1% of the time, Pallas kernels for 0%

commit v1 on v0

v1 whole, which is shorter than its diff:
```python
import functools
import math
import numpy as np
import jax
import jax.numpy as jnp
from jax import lax
from jax.experimental import pallas as pl
from jax.experimental.pallas import tpu as pltpu
from jax.sharding import PartitionSpec as P

NORM_EPS = 1e-5
ROPE_THETA = 500000.0
MASK_VALUE = -1e30
MESH = pl.DeviceIdType.MESH
BF16 = jnp.bfloat16
F32 = jnp.float32

BATCH = 8
HEAD = 128
HEADS = 10
GROUPS = 2
PER = HEADS // GROUPS
HID = 5120
BLK = 1280
QW = HEADS * HEAD
KVW = GROUPS * HEAD
FFW = 896
FF_TILES = 27
SLOTS = 256
TOK = 1601
VMEM_LIMIT = 67043328
PIECE = 640
SCALE = HEAD ** -0.5
N_LOCAL = 64
N_REMOTE = 48


def rope_freqs(head_dim):
    freq_list = []
    for index in range(head_dim // 2):
        base_freq = 1.0 / (ROPE_THETA ** (2.0 * index / head_dim))
        wave_len = 2.0 * math.pi / base_freq
        if wave_len < 2048.0:
            freq_list.append(base_freq)
        elif wave_len > 8192.0:
            freq_list.append(base_freq / 8.0)
        else:
            smooth = (8192.0 / wave_len - 1.0) / 3.0
            freq_list.append((1.0 - smooth) * base_freq / 8.0 + smooth * base_freq)
    return np.array(freq_list + freq_list, dtype=np.float32)


def dot(a, b):
    return jnp.dot(a, b, preferred_element_type=F32)


def bf(value):
    return value.astype(BF16).astype(F32)


def kernel(x_h, gains_h, rope_h, gates_ref, seq_ref, vis_h,
           ks_h, vs_h, kx_h, vx_h,
           wq1_h, wk_h, wv_h, wo1_h, wg1_h, wu1_h, wd1_h,
           wq2_h, wo2_h, wg2_h, wu2_h, wd2_h,
           h_out, k_out, v_out,
           x_v, gains_v, rope_v, vis_v, buf_a, buf_o,
           u_v, qbd_v, o_v, s_self, p_self, s_cross, p_cross,
           comb, part, rs_buf, hs_buf, y_buf, zs_buf, zr_buf, t_buf, ty_buf, hbuf,
           lsem, wsem, send_sem, recv_sem):
    tp = lax.axis_index("tp")
    kv = lax.axis_index("kv")
    core = lax.rem(tp, 2)
    mate_tp = tp + 1 - 2 * core
    mate = {"tp": mate_tp}
    across = {"tp": lax.rem(tp + 2, 4)}
    around = [lax.rem(kv + j, 4) for j in (3, 2, 1)]
    counts = {"remote": 0, "local": 0}

    def remote(src, dst, device):
        i = counts["remote"]
        counts["remote"] += 1
        copy = pltpu.make_async_remote_copy(src_ref=src, dst_ref=dst, send_sem=send_sem.at[i],
                                            recv_sem=recv_sem.at[i], device_id=device, device_id_type=MESH)
        copy.start()
        return copy

    def local(src, dst):
        i = counts["local"]
        counts["local"] += 1
        copy = pltpu.make_async_copy(src, dst, lsem.at[i])
        copy.start()
        return copy

    def wait_all(copies):
        for copy in copies:
            copy.wait()

    ff_off = pl.multiple_of(jnp.minimum(kv * 7, FF_TILES - 7) * 128, 128)

    def copy_a(w_h, c):
        return pltpu.make_async_copy(w_h.at[pl.ds(c * BLK, BLK), :], buf_a.at[c], wsem.at[c])

    def copies_a(w_h):
        return [copy_a(w_h, c) for c in range(4)]

    def copies_o(w_h):
        return [pltpu.make_async_copy(w_h.at[:, pl.ds(c * BLK, BLK)], buf_o.at[c], wsem.at[4 + c]) for c in range(4)]

    def copies_up(wg_h, wu_h, gu):
        return [pltpu.make_async_copy(w_h.at[pl.ds(c * BLK, BLK), pl.ds(ff_off, FFW)], gu.at[c, :, pl.ds(i * FFW, FFW)],
                                      wsem.at[8 + 2 * c + i]) for c in range(4) for i, w_h in enumerate((wg_h, wu_h))]

    def copies_down(wd_h, dn):
        return [pltpu.make_async_copy(wd_h.at[pl.ds(ff_off, FFW), pl.ds(c * BLK, BLK)], dn.at[c], wsem.at[16 + c])
                for c in range(4)]

    def start_all(copies):
        for copy in copies:
            copy.start()

    first = [local(x_h, x_v), local(gains_h, gains_v), local(rope_h, rope_v), local(vis_h, vis_v)]
    rows = lax.broadcasted_iota(jnp.int32, (BATCH, 1), 0)
    lanes = lax.broadcasted_iota(jnp.int32, (BATCH, HEAD), 1)
    seq = jnp.zeros((BATCH, 1), jnp.int32)
    for b in range(BATCH):
        seq = jnp.where(rows == b, seq_ref[b], seq)

    def norm_to_u(slot, gain_row):
        total = jnp.zeros((BATCH, 1), F32)
        for p in range(8):
            h = hbuf[slot, p]
            total = total + jnp.sum(h * h, axis=-1, keepdims=True)
        scale = lax.rsqrt(total / HID + NORM_EPS)
        for p in range(8):
            u_v[p] = hbuf[slot, p] * scale * gains_v[gain_row:gain_row + 1, p * PIECE:(p + 1) * PIECE]

    def u_block(c):
        return jnp.concatenate([u_v[2 * c], u_v[2 * c + 1]], axis=-1).astype(BF16)

    def put_queries(query):
        zero = jnp.zeros((BATCH, HEAD), F32)
        for r in range(HEADS):
            g = r // PER
            qbd_v[r * BATCH:(r + 1) * BATCH, g * HEAD:(g + 1) * HEAD] = query[r]
            qbd_v[r * BATCH:(r + 1) * BATCH, (1 - g) * HEAD:(2 - g) * HEAD] = zero

    def scores(keys, s_ref):
        q = qbd_v[...].astype(BF16)
        for b in range(BATCH):
            k_cat = jnp.concatenate([keys[b, 0], keys[b, 1]], axis=-1)
            s = lax.dot_general(q, k_cat, (((1,), (1,)), ((), ())), preferred_element_type=F32)
            for r in range(HEADS):
                s_ref[r, b:b + 1, :] = s[r * BATCH + b:r * BATCH + b + 1, :]

    def weigh(values, p_ref):
        for b in range(BATCH):
            v_cat = jnp.concatenate([values[b, 0], values[b, 1]], axis=-1)
            o = dot(p_ref[...], v_cat)
            for r in range(HEADS):
                g = r // PER
                o_v[r, b:b + 1, :] = o[r * BATCH + b:r * BATCH + b + 1, g * HEAD:(g + 1) * HEAD]

    def put_partials(slot, outs, tops, totals):
        top_row = jnp.full((BATCH, HEAD), MASK_VALUE, F32)
        total_row = jnp.zeros((BATCH, HEAD), F32)
        for r in range(HEADS):
            comb[slot, kv, :, r * HEAD:(r + 1) * HEAD] = outs[r]
            top_row = jnp.where(lanes == r, tops[r], top_row)
            total_row = jnp.where(lanes == r, totals[r], total_row)
        comb[slot, kv, :, QW:QW + HEAD] = top_row
        comb[slot, kv, :, QW + HEAD:QW + 2 * HEAD] = total_row

    def exchange_partials(slot):
        wait_all([remote(comb.at[slot, kv], comb.at[slot, kv], {"kv": peer}) for peer in around])
        best = comb[slot, 0, :, QW:QW + HEAD]
        for s in range(1, 4):
            best = jnp.maximum(best, comb[slot, s, :, QW:QW + HEAD])
        weight = [jnp.exp(comb[slot, s, :, QW:QW + HEAD] - best) for s in range(4)]
        norm = sum(comb[slot, s, :, QW + HEAD:QW + 2 * HEAD] * weight[s] for s in range(4))
        inverse = 1.0 / jnp.where(norm > 0, norm, 1.0)
        heads = []
        for r in range(HEADS):
            mixed = sum(comb[slot, s, :, r * HEAD:(r + 1) * HEAD] * weight[s][:, r:r + 1] for s in range(4))
            heads.append(mixed * inverse[:, r:r + 1])
        return jnp.concatenate(heads, axis=-1).astype(BF16)

    def halves(slot, left, w_ref):
        def run(base):
            def body(i, carry):
                out = dot(left, w_ref[base + i])
                part[slot, 2 * (base + i)] = out[:, :PIECE]
                part[slot, 2 * (base + i) + 1] = out[:, PIECE:]
                return carry
            lax.fori_loop(0, 2, body, 0)
        run(2 * (1 - core))
        copy = remote(part.at[slot, pl.ds(4 * (1 - core), 4)], rs_buf.at[slot], mate)
        run(2 * core)
        copy.wait()

    def reduce_plane(slot, i_h, h_from, h_to, finish):
        sends = []
        for i in range(2):
            for j in (2 * i, 2 * i + 1):
                hs_buf[i_h, j] = part[slot, 4 * core + j] + rs_buf[slot, j]
            sends.append(remote(hs_buf.at[i_h, pl.ds(2 * i, 2)], y_buf.at[i_h, pl.ds(2 * i, 2)], across))
        backs = []
        for i in range(2):
            sends[i].wait()
            for j in (2 * i, 2 * i + 1):
                p = 4 * core + j
                hbuf[h_to, p] = bf(finish(hbuf[h_from, p], hs_buf[i_h, j] + y_buf[i_h, j]))
            span = hbuf.at[h_to, pl.ds(4 * core + 2 * i, 2)]
            backs.append(remote(span, span, mate))
        wait_all(backs)

    def reduce_all(slot, i_z, h_from, h_to, finish):
        for j in range(4):
            zs_buf[i_z, j] = part[slot, 4 * core + j] + rs_buf[slot, j]
        copies = [remote(zs_buf.at[i_z, peer], zr_buf.at[i_z, kv], {"kv": peer}) for peer in around]
        zr_buf[i_z, kv] = zs_buf[i_z, kv]
        wait_all(copies)
        t_buf[i_z] = zr_buf[i_z, 0] + zr_buf[i_z, 1] + zr_buf[i_z, 2] + zr_buf[i_z, 3]
        remote(t_buf.at[i_z], ty_buf.at[i_z], across).wait()
        p = 4 * core + kv
        hbuf[h_to, p] = bf(finish(hbuf[h_from, p], t_buf[i_z] + ty_buf[i_z]))
        own = hbuf.at[h_to, p]
        copies = []
        for peer in around:
            copies.append(remote(own, own, {"kv": peer}))
            copies.append(remote(own, own, {"kv": peer, "tp": mate_tp}))
        copies.append(remote(own, own, mate))
        wait_all(copies)

    def mlp(slot, gain_row, h_slot, gu, dn, up, down):
        norm_to_u(h_slot, gain_row)
        acc = jnp.zeros((BATCH, 2 * FFW), F32)
        for c in range(4):
            wait_all(up[2 * c:2 * c + 2])
            acc = acc + dot(u_block(c), gu[c])
        gate, upper = acc[:, :FFW], acc[:, FFW:]
        act = gate * (1.0 / (1.0 + jnp.exp(-gate))) * upper
        keep = jnp.logical_or(kv < 3, lax.broadcasted_iota(jnp.int32, (BATCH, FFW), 1) >= 128)
        act = jnp.where(keep, act, 0.0).astype(BF16)
        wait_all(down)
        halves(slot, act, dn)

    start_all(copies_a(wq1_h))

    def self_attention(wkv, ks, vs, gu):
        w_kv = [(local(wk_h.at[pl.ds(c * BLK, BLK), :], wkv.at[c, :, pl.ds(0, KVW)]),
                 local(wv_h.at[pl.ds(c * BLK, BLK), :], wkv.at[c, :, pl.ds(KVW, KVW)])) for c in range(4)]
        caches = [local(ks_h, ks), local(vs_h, vs)]
        start_all(copies_o(wo1_h))
        start_all(copies_up(wg1_h, wu1_h, gu))

        barrier = pltpu.get_barrier_semaphore()
        peers = [{"kv": peer} for peer in around] + [{"kv": peer, "tp": mate_tp} for peer in around] + [mate, across]
        for peer in peers:
            pl.semaphore_signal(barrier, inc=1, device_id=peer, device_id_type=MESH)

        wait_all(first)
        for p in range(8):
            hbuf[0, p] = x_v[:, p * PIECE:(p + 1) * PIECE].astype(F32)
        norm_to_u(0, 0)
        angles = seq.astype(F32) * rope_v[0:1, :]
        cos_t = jnp.cos(angles)
        sin_t = jnp.sin(angles) * jnp.where(lanes < HEAD // 2, -1.0, 1.0)

        def rope(z):
            return bf(z * cos_t + pltpu.roll(z, HEAD // 2, 1) * sin_t)

        acc_q = jnp.zeros((BATCH, QW), F32)
        acc_kv = jnp.zeros((BATCH, 2 * KVW), F32)
        for c in range(4):
            copy_a(wq1_h, c).wait()
            wait_all(w_kv[c])
            left = u_block(c)
            acc_q = acc_q + dot(left, buf_a[c])
            acc_kv = acc_kv + dot(left, wkv[c])
        query = [rope(acc_q[:, r * HEAD:(r + 1) * HEAD]) for r in range(HEADS)]
        key_new = [rope(acc_kv[:, g * HEAD:(g + 1) * HEAD]) for g in range(GROUPS)]
        val_new = [bf(acc_kv[:, KVW + g * HEAD:KVW + (g + 1) * HEAD]) for g in range(GROUPS)]
        for g in range(GROUPS):
            k_out[:, g * HEAD:(g + 1) * HEAD] = key_new[g].astype(BF16)
            v_out[:, g * HEAD:(g + 1) * HEAD] = val_new[g].astype(BF16)
        put_queries(query)
        wait_all(caches)
        scores(ks, s_self)
        slot_ids = kv * SLOTS + lax.broadcasted_iota(jnp.int32, (BATCH, SLOTS), 1)
        visible = slot_ids < seq
        owner = jnp.logical_and(seq >= kv * SLOTS, seq < (kv + 1) * SLOTS)
        tops, totals, news = [], [], []
        for pair in range(HEADS // 2):
            both = []
            for r in (2 * pair, 2 * pair + 1):
                s = jnp.where(visible, s_self[r] * SCALE, MASK_VALUE)
                new = jnp.sum(query[r] * key_new[r // PER], axis=-1, keepdims=True) * SCALE
                new = jnp.where(owner, new, MASK_VALUE)
                top = jnp.maximum(jnp.max(s, axis=-1, keepdims=True), new)
                prob = jnp.where(visible, jnp.exp(s - top), 0.0)
                new_prob = jnp.where(owner, jnp.exp(new - top), 0.0)
                tops.append(top)
                totals.append(jnp.sum(prob, axis=-1, keepdims=True) + new_prob)
                news.append(new_prob)
                both.append(prob)
            p_self[2 * pair * BATCH:(2 * pair + 2) * BATCH, :] = jnp.concatenate(both, axis=0).astype(BF16)
        weigh(vs, p_self)
        outs = [o_v[r] + news[r] * val_new[r // PER] for r in range(HEADS)]
        pl.semaphore_wait(barrier, len(peers))
        put_partials(0, outs, tops, totals)

    def self_rest(dn, gu):
        start_all(copies_down(wd1_h, dn))
        start_all(copies_a(wq2_h))
        attn = exchange_partials(0)
        wait_all(copies_o(wo1_h))
        halves(0, attn, buf_o)
        start_all(copies_o(wo2_h))
        reduce_plane(0, 0, 0, 1, lambda h, s: h + s)
        mlp(1, 1, 1, gu, dn, copies_up(wg1_h, wu1_h, gu), copies_down(wd1_h, dn))

    up_space = pltpu.VMEM((4, BLK, 2 * FFW), BF16)
    down_space = pltpu.VMEM((4, FFW, BLK), BF16)

    def phase_one(gu):
        pl.run_scoped(functools.partial(self_attention, gu=gu), pltpu.VMEM((4, BLK, 2 * KVW), BF16),
                      pltpu.VMEM((BATCH, GROUPS, SLOTS, HEAD), BF16), pltpu.VMEM((BATCH, GROUPS, SLOTS, HEAD), BF16))
        pl.run_scoped(functools.partial(self_rest, gu=gu), down_space)

    pl.run_scoped(phase_one, up_space)

    visible_tile = jnp.sum(jnp.where(lax.broadcasted_iota(jnp.int32, (BATCH, 4), 1) == kv, vis_v[...], 0),
                           axis=-1, keepdims=True) > 0
    row_on = jnp.where(jnp.sum(vis_v[...], axis=-1, keepdims=True) > 0, 1.0, 0.0)

    def scope_two(kx, vx):
        caches = [local(kx_h, kx), local(vx_h, vx)]
        reduce_all(1, 0, 1, 2, lambda h, s: h + s)
        norm_to_u(2, 2)
        acc = jnp.zeros((BATCH, QW), F32)
        for c in range(4):
            copy_a(wq2_h, c).wait()
            acc = acc + dot(u_block(c), buf_a[c])
        query = []
        for r in range(HEADS):
            z = acc[:, r * HEAD:(r + 1) * HEAD]
            z = z * lax.rsqrt(jnp.mean(z * z, axis=-1, keepdims=True) + NORM_EPS) * gains_v[4:5, 0:HEAD]
            query.append(bf(z))
        put_queries(query)
        wait_all(caches)
        scores(kx, s_cross)
        tops, totals = [], []
        for pair in range(HEADS // 2):
            both = []
            for r in (2 * pair, 2 * pair + 1):
                s = s_cross[r] * SCALE
                top = jnp.max(s, axis=-1, keepdims=True)
                prob = jnp.exp(s - top)
                tops.append(jnp.where(visible_tile, top, MASK_VALUE))
                totals.append(jnp.where(visible_tile, jnp.sum(prob, axis=-1, keepdims=True), 0.0))
                both.append(prob)
            p_cross[2 * pair * BATCH:(2 * pair + 2) * BATCH, :] = jnp.concatenate(both, axis=0).astype(BF16)
        weigh(vx, p_cross)
        outs = [jnp.where(visible_tile, o_v[r], 0.0) for r in range(HEADS)]
        put_partials(1, outs, tops, totals)

    pl.run_scoped(scope_two, pltpu.VMEM((BATCH, GROUPS, TOK, HEAD), BF16), pltpu.VMEM((BATCH, GROUPS, TOK, HEAD), BF16))

    def gate(i):
        return jnp.tanh(jnp.full((BATCH, HEAD), gates_ref[i], F32))[:, 0:1] * row_on

    def scope_three(gu, dn):
        start_all(copies_up(wg2_h, wu2_h, gu))
        start_all(copies_down(wd2_h, dn))
        attn = exchange_partials(1)
        wait_all(copies_o(wo2_h))
        halves(2, attn, buf_o)
        reduce_plane(2, 1, 2, 3, lambda h, s: h + gate(0) * s)
        mlp(3, 3, 3, gu, dn, copies_up(wg2_h, wu2_h, gu), copies_down(wd2_h, dn))

    pl.run_scoped(scope_three, up_space, down_space)
    reduce_all(3, 1, 3, 4, lambda h, s: h + gate(1) * s)
    for p in range(8):
        h_out[:, p * PIECE:(p + 1) * PIECE] = hbuf[4, p].astype(BF16)


def solution(mesh):
    rows_spec = P('dp', None)
    cache_spec = P('dp', 'tp', 'kv', None)
    new_spec = P('dp', 'tp', None)
    col_spec = P(None, 'tp')
    row_spec = P('tp', None)
    vec_spec = P(None)
    in_specs = (rows_spec, cache_spec, cache_spec, P('dp'), cache_spec, cache_spec, rows_spec,
                vec_spec, col_spec, col_spec, col_spec, row_spec, vec_spec, col_spec, col_spec, row_spec,
                vec_spec, col_spec, vec_spec, row_spec, vec_spec, vec_spec, col_spec, col_spec, row_spec)
    out_specs = (rows_spec, new_spec, new_spec)

    def device_step(x, ks_cache, vs_cache, seq_len, kx_cache, vx_cache, tile_vis, attn_norm, wq_self, wk_self, wv_self, wo_self, mlp_norm, wg_self, wu_self, wd_self, xattn_norm, wq_cross, q_norm, wo_cross, cross_gates, xmlp_norm, wg_cross, wu_cross, wd_cross):
        gains = jnp.stack([attn_norm, mlp_norm, xattn_norm, xmlp_norm, jnp.pad(q_norm, (0, HID - HEAD))]
                          + [jnp.zeros_like(attn_norm)] * 3).astype(F32)
        freqs = jnp.tile(jnp.asarray(rope_freqs(HEAD))[None, :], (8, 1))
        hbm = pl.BlockSpec(memory_space=pl.ANY)
        smem = pl.BlockSpec(memory_space=pltpu.SMEM)
        vmem = pl.BlockSpec(memory_space=pltpu.VMEM)
        piece = (8, BATCH, PIECE)
        scratch = [
            pltpu.VMEM((BATCH, HID), BF16), pltpu.VMEM((8, HID), F32), pltpu.VMEM((8, HEAD), F32), pltpu.VMEM((BATCH, 4), jnp.int32),
            pltpu.VMEM((4, BLK, BLK), BF16), pltpu.VMEM((4, BLK, BLK), BF16),
            pltpu.VMEM(piece, F32), pltpu.VMEM((HEADS * BATCH, 2 * HEAD), F32), pltpu.VMEM((HEADS, BATCH, HEAD), F32),
            pltpu.VMEM((HEADS, BATCH, SLOTS), F32), pltpu.VMEM((HEADS * BATCH, SLOTS), BF16),
            pltpu.VMEM((HEADS, BATCH, TOK), F32), pltpu.VMEM((HEADS * BATCH, TOK), BF16),
            pltpu.VMEM((2, 4, BATCH, QW + 2 * HEAD), F32),
            pltpu.VMEM((4,) + piece, F32), pltpu.VMEM((4, 4, BATCH, PIECE), F32),
            pltpu.VMEM((2, 4, BATCH, PIECE), F32), pltpu.VMEM((2, 4, BATCH, PIECE), F32),
            pltpu.VMEM((2, 4, BATCH, PIECE), F32), pltpu.VMEM((2, 4, BATCH, PIECE), F32),
            pltpu.VMEM((2, BATCH, PIECE), F32), pltpu.VMEM((2, BATCH, PIECE), F32),
            pltpu.VMEM((5,) + piece, F32),
            pltpu.SemaphoreType.DMA((N_LOCAL,)), pltpu.SemaphoreType.DMA((20,)), pltpu.SemaphoreType.DMA((N_REMOTE,)), pltpu.SemaphoreType.DMA((N_REMOTE,)),
        ]
        h, key_new, val_new = pl.pallas_call(
            kernel,
            out_shape=(jax.ShapeDtypeStruct((BATCH, HID), BF16), jax.ShapeDtypeStruct((BATCH, KVW), BF16),
                       jax.ShapeDtypeStruct((BATCH, KVW), BF16)),
            in_specs=[hbm, hbm, hbm, smem, smem, hbm] + [hbm] * 16,
            out_specs=(vmem, vmem, vmem),
            scratch_shapes=scratch,
            compiler_params=pltpu.CompilerParams(collective_id=0, has_side_effects=True, vmem_limit_bytes=VMEM_LIMIT),
        )(x, gains, freqs, cross_gates, seq_len, tile_vis, ks_cache, vs_cache, kx_cache, vx_cache,
          wq_self, wk_self, wv_self, wo_self, wg_self, wu_self, wd_self, wq_cross, wo_cross, wg_cross, wu_cross, wd_cross)
        return h, key_new.reshape(BATCH, GROUPS, HEAD), val_new.reshape(BATCH, GROUPS, HEAD)

    return jax.shard_map(device_step, mesh=mesh, in_specs=in_specs, out_specs=out_specs, check_vma=False)
```

time: 306 us -> 105 us (0.34)
  waiting for transfers between devices: 126 us -> 0 us
  matrix products: 120 us -> 0 us
  Pallas kernels: 0 us -> 83.2 us
  blocking collectives: 30 us -> 0 us
  local copies, waits for them, and re-layouts: 2.76 us -> 20.1 us
  between operations: 14.1 us -> 0.69 us
  other arithmetic: 12.2 us -> 0.68 us
    psum x4 -> x0, waiting for transfers between devices: 126 us -> none  [the longest x1 33 us: device_step(): lax.psum(jnp.dot(attn_self, wo_self, preferred_element_type=jnp.float32),...]
    dot_general x15 -> x0, matrix products: 120 us -> none  [the longest x2 50.7 us: swiglu_part(): return jnp.dot(hidden_act, w_down, preferred_element_type=jnp.float32)]
    pallas_call x0 -> x1, Pallas kernels: none -> 83.2 us  [device_step(): pl.pallas_call(kernel, out_shape=(jax.ShapeDtypeStruct((BATCH, HID), BF16...]
    all_gather x2 -> x0, blocking collectives: 30 us -> none  [combine_partials(): gathered = lax.all_gather(packed, 'kv', axis=0)]
    unnamed x25 -> x12, local copies, waits for them, and re-layouts: 0.68 us -> 15.7 us
    reduce_sum x10 -> x0, other arithmetic: 5.11 us -> none  [the longest x4 4.32 us: rms_norm(): jnp.mean(hidden * hidden, axis=-1, keepdims=True) + NORM_EPS]
    another operation x0 -> x9, local copies, waits for them, and re-layouts: none -> 3.72 us  [the longest x8 3.13 us: device_step(): jnp.stack([attn_norm, mlp_norm, xattn_norm, xmlp_norm, jnp.pad(q_norm, (0...]
  transfers between devices with their start and end apart: 4 -> 0, of which waited for: 4 -> 0; matrix products, arithmetic and copies ran while one was open for 1% -> 0% of each run, Pallas kernels for 0% -> 0%
where the time goes in v1:
time: 105 us
  Pallas kernels  83.2 us (79%)
  local copies, waits for them, and re-layouts  20.1 us (19%)
    pallas_call x1, Pallas kernels, device_step(): pl.pallas_call(kernel, out_shape=(jax.ShapeDtypeStruct((BATCH, HID), BF16...  83.2 us
    unnamed x12, local copies, waits for them, and re-layouts  15.7 us
    another operation x8, local copies, waits for them, and re-layouts, device_step(): jnp.stack([attn_norm, mlp_norm, xattn_norm, xmlp_norm, jnp.pad(q_norm, (0...  3.13 us

profile of v1, /device:TPU:0, one launch (start us, length us, event | category | flops | bytes accessed | tf_op | source)
XLA Modules:
  0.0 104.7 jit_solution(12355817611276778120)
XLA Ops:
  0.6 0.0 slice-start
  0.6 1.5 %copy.29.vis_h = s32[8,4]{1,0:T(8,128)} copy(s32[8,4]{0,1:T(4,128)} %param.32) | data formatting | bytes 256 | tf_op args[6]
  2.1 0.7 pad.4
  2.8 0.7 stack.21
  3.5 0.7 stack.22
  4.3 0.7 stack.23
  5.0 0.7 stack.24
  5.7 0.2 stack.27
  6.0 0.7 convert_element_type.5.gains_h
  6.6 0.0 slice-start.1
  6.6 0.0 copy-start
  6.7 6.6 %copy.30.kx_h = bf16[8,2,1601,128]{3,2,1,0:T(8,128)(2,1)} copy(bf16[8,2,1601,128]{3,1,2,0:T(2,128)(2,1)} %param.30) | data formatting | bytes 13115392 | tf_op args[4]
  13.2 0.0 slice-done
  13.3 0.0 slice-done.1
  13.3 3.6 %copy.31.vx_h = bf16[8,2,1601,128]{3,2,1,0:T(8,128)(2,1)} copy(bf16[8,2,1601,128]{3,1,2,0:T(2,128)(2,1)S(1)} %bitcast.3) | data formatting | bytes 13115392 | tf_op args[5]
  16.8 0.0 copy-done
  16.8 0.6 tile.2.rope_h
  17.4 83.2 %shard_map.265 = (bf16[8,5120]{1,0:T(8,128)(2,1)}, bf16[8,256]{1,0:T(8,128)(2,1)}, bf16[8,256]{1,0:T(8,128)(2,1)}) custom-call(bf16[8,5120]{1,0:T(8,128)(2,1)} %x_h.1, f32[8,5120]{1,0:T(8,128)} %convert_element_type.5.gains_h, f32[8,128]{1,0:T(8,128)} %tile.2.rope_h, f32[2]{0:T(128)} %gates_ref.1, s32[8]{0:T(128)} %seq_ref.1, s32[8,4]{1,0:T(8,128)} %copy.29.vis_h, ...), custom_call_target="tpu_custom_call" | custom-call | tf_op jit(solution)/shard_map/pallas_call | solution.py:421
  100.6 1.3 %copy.32 = bf16[8,2,128]{2,1,0:T(2,128)(2,1)} copy(bf16[8,2,128]{2,0,1:T(8,128)(2,1)} %bitcast.5) | data formatting | bytes 8192
  101.9 1.3 %copy.33 = bf16[8,2,128]{2,1,0:T(2,128)(2,1)} copy(bf16[8,2,128]{2,0,1:T(8,128)(2,1)} %bitcast.4) | data formatting | bytes 8192
  103.2 1.5 %copy.35 = bf16[8,5120]{1,0:T(8,128)(2,1)} copy(bf16[8,5120]{1,0:T(8,128)(2,1)} %get-tuple-element.15) | data formatting | bytes 163840
  (4 shorter events, 0.0 us)
Async XLA Ops:
  0.6 12.6 %slice-start = ((s8[6557696]{0:T(1024)(128)(4,1)}), s8[2363392]{0:T(1024)(128)(4,1)S(1)}, s32[]{:S(2)}) async-start(s8[6557696]{0:T(1024)(128)(4,1)} %bitcast.2), calls=%async_computation | async-start | bytes 4726784
  6.6 6.6 %slice-start.1 = ((s8[6557696]{0:T(1024)(128)(4,1)}), s8[4194304]{0:T(1024)(128)(4,1)S(1)}, s32[]{:S(2)}) async-start(s8[6557696]{0:T(1024)(128)(4,1)} %bitcast.2), calls=%async_computation.1 | async-start | bytes 8388608
  6.6 10.2 %copy-start = (f32[128]{0:T(128)S(1)}, f32[128]{0:T(128)}, u32[]{:S(2)}) copy-start(f32[128]{0:T(128)} %constant.3.clone) | copy-start | bytes 1540

commit v2 on v1

v2 whole, which is shorter than its diff:
```python
import functools
import math
import numpy as np
import jax
import jax.numpy as jnp
from jax import lax
from jax.experimental import pallas as pl
from jax.experimental.pallas import tpu as pltpu
from jax.sharding import PartitionSpec as P

NORM_EPS = 1e-5
ROPE_THETA = 500000.0
MASK_VALUE = -1e30
MESH = pl.DeviceIdType.MESH
BF16 = jnp.bfloat16
F32 = jnp.float32

BATCH = 8
HEAD = 128
HEADS = 10
GROUPS = 2
PER = HEADS // GROUPS
HID = 5120
BLK = 1280
QW = HEADS * HEAD
KVW = GROUPS * HEAD
FFW = 896
FF_TILES = 27
SLOTS = 256
TOK = 1601
ROWS = 2 * TOK * BATCH
STEP = 2 * TOK - 2
WIN = STEP + 16
VMEM_LIMIT = 67043328
PIECE = 640
SCALE = HEAD ** -0.5
N_LOCAL = 11
N_REMOTE = 29


def rope_freqs(head_dim):
    freq_list = []
    for index in range(head_dim // 2):
        base_freq = 1.0 / (ROPE_THETA ** (2.0 * index / head_dim))
        wave_len = 2.0 * math.pi / base_freq
        if wave_len < 2048.0:
            freq_list.append(base_freq)
        elif wave_len > 8192.0:
            freq_list.append(base_freq / 8.0)
        else:
            smooth = (8192.0 / wave_len - 1.0) / 3.0
            freq_list.append((1.0 - smooth) * base_freq / 8.0 + smooth * base_freq)
    return np.array(freq_list + freq_list, dtype=np.float32)


def cos_sin(angle):
    turns = jnp.floor(angle * (2.0 / math.pi) + 0.5)
    r = ((angle - turns * 1.5703125) - turns * 4.837512969970703125e-4) - turns * 7.54978995489188216e-8
    z = r * r
    s = r + r * z * ((-1.9515295891e-4 * z + 8.3321608736e-3) * z - 1.6666654611e-1)
    c = 1.0 - 0.5 * z + z * z * ((2.443315711809948e-5 * z - 1.388731625493765e-3) * z + 4.166664568298827e-2)
    quarter = turns - 4.0 * jnp.floor(turns * 0.25)
    swap = jnp.logical_or(quarter == 1.0, quarter == 3.0)
    cos_t = jnp.where(swap, s, c) * jnp.where(jnp.logical_or(quarter == 1.0, quarter == 2.0), -1.0, 1.0)
    sin_t = jnp.where(swap, c, s) * jnp.where(quarter >= 2.0, -1.0, 1.0)
    return cos_t, sin_t


def dot(a, b):
    return jnp.dot(a, b, preferred_element_type=F32)


def bf(value):
    return value.astype(BF16).astype(F32)


def kernel(x_h, n0_h, n1_h, n2_h, n3_h, qn_h, rope_h, gates_ref, seq_ref, vis_ref,
           ks_h, vs_h, kx_h, vx_h,
           wq1_h, wk_h, wv_h, wo1_h, wg1_h, wu1_h, wd1_h,
           wq2_h, wo2_h, wg2_h, wu2_h, wd2_h,
           h_out, k_out, v_out,
           x_v, kv_v, raw_v, qn_v, gains_v, rope_v, buf_a, buf_o,
           u_v, qbd_v, qc_v, o_v, s_self, p_self, s_cross, p_cross,
           comb, part, rs_buf, hs_buf, y_buf, zr_buf, gather, hbuf,
           lsem, wsem, osem, send_sem, recv_sem):
    tp = lax.axis_index("tp")
    kv = lax.axis_index("kv")
    core = lax.rem(tp, 2)
    side = tp // 2
    mate = {"tp": tp + 1 - 2 * core}
    across = {"tp": lax.rem(tp + 2, 4)}
    around = [lax.rem(kv + j, 4) for j in (3, 2, 1)]
    counts = {"remote": 0, "local": 0}

    def remote(src, dst, device):
        i = counts["remote"]
        counts["remote"] += 1
        copy = pltpu.make_async_remote_copy(src_ref=src, dst_ref=dst, send_sem=send_sem.at[i],
                                            recv_sem=recv_sem.at[i], device_id=device, device_id_type=MESH)
        copy.start()
        return copy

    def local(src, dst):
        i = counts["local"]
        counts["local"] += 1
        copy = pltpu.make_async_copy(src, dst, lsem.at[i])
        copy.start()
        return copy

    def wait_all(copies):
        for copy in copies:
            copy.wait()

    ff_off = pl.multiple_of(jnp.minimum(kv * 7, FF_TILES - 7) * 128, 128)

    def copy_a(w_h, c):
        return pltpu.make_async_copy(w_h.at[pl.ds(c * BLK, BLK), :], buf_a.at[c], wsem.at[c])

    def copies_a(w_h):
        return [copy_a(w_h, c) for c in range(4)]

    def copy_o(w_h, c):
        return pltpu.make_async_copy(w_h.at[:, pl.ds(c * BLK, BLK)], buf_o.at[c], wsem.at[4 + c])

    def copies_o(w_h):
        return [copy_o(w_h, c) for c in range(4)]

    def copies_up(wg_h, wu_h, gu):
        return [pltpu.make_async_copy(w_h.at[pl.ds(c * BLK, BLK), pl.ds(ff_off, FFW)], gu.at[c, :, pl.ds(i * FFW, FFW)],
                                      wsem.at[8 + 2 * c + i]) for c in range(4) for i, w_h in enumerate((wg_h, wu_h))]

    def copies_down(wd_h, dn):
        return [pltpu.make_async_copy(wd_h.at[pl.ds(ff_off, FFW), pl.ds(c * BLK, BLK)], dn.at[c], wsem.at[16 + c])
                for c in range(4)]

    def start_all(copies):
        for copy in copies:
            copy.start()

    first = [local(x_h, x_v), local(n0_h, raw_v.at[0]), local(rope_h, rope_v.at[0])]
    later = [local(n1_h, raw_v.at[1]), local(n2_h, raw_v.at[2]), local(n3_h, raw_v.at[3]), local(qn_h, qn_v)]
    rows = lax.broadcasted_iota(jnp.int32, (BATCH, 1), 0)
    lanes = lax.broadcasted_iota(jnp.int32, (BATCH, HEAD), 1)
    seq = jnp.zeros((BATCH, 1), jnp.int32)
    for b in range(BATCH):
        seq = jnp.where(rows == b, seq_ref[b], seq)
    seen_here = jnp.zeros((BATCH, 1), jnp.int32)
    seen = jnp.zeros((BATCH, 1), jnp.int32)
    for b in range(BATCH):
        seen_here = jnp.where(rows == b, vis_ref[kv, b], seen_here)
        seen = jnp.where(rows == b, vis_ref[0, b] + vis_ref[1, b] + vis_ref[2, b] + vis_ref[3, b], seen)

    def norm_to_u(slot, gain_row):
        total = jnp.zeros((BATCH, 1), F32)
        for p in range(8):
            h = hbuf[slot, p]
            total = total + jnp.sum(h * h, axis=-1, keepdims=True)
        scale = lax.rsqrt(total / HID + NORM_EPS)
        for p in range(8):
            for i in range(5):
                span = slice(i * HEAD, (i + 1) * HEAD)
                row = 5 * p + i
                u_v[p, :, span] = hbuf[slot, p, :, span] * scale * gains_v[gain_row, row:row + 1, :]

    def u_block(c):
        return jnp.concatenate([u_v[2 * c], u_v[2 * c + 1]], axis=-1).astype(BF16)

    def put_queries(query):
        zero = jnp.zeros((BATCH, HEAD), F32)
        for r in range(HEADS):
            g = r // PER
            qbd_v[r * BATCH:(r + 1) * BATCH, g * HEAD:(g + 1) * HEAD] = query[r]
            qbd_v[r * BATCH:(r + 1) * BATCH, (1 - g) * HEAD:(2 - g) * HEAD] = zero

    def scores(keys, s_ref):
        q = qbd_v[...].astype(BF16)
        for b in range(BATCH):
            k_cat = jnp.concatenate([keys[b, 0], keys[b, 1]], axis=-1)
            s = lax.dot_general(q, k_cat, (((1,), (1,)), ((), ())), preferred_element_type=F32)
            for r in range(HEADS):
                s_ref[r, b:b + 1, :] = s[r * BATCH + b:r * BATCH + b + 1, :]

    def weigh(values, p_ref):
        for b in range(BATCH):
            v_cat = jnp.concatenate([values[b, 0], values[b, 1]], axis=-1)
            o = dot(p_ref[...], v_cat)
            for r in range(HEADS):
                g = r // PER
                o_v[r, b:b + 1, :] = o[r * BATCH + b:r * BATCH + b + 1, g * HEAD:(g + 1) * HEAD]

    def put_partials(slot, outs, tops, totals):
        stats = jnp.zeros((BATCH, HEAD), F32)
        for r in range(HEADS):
            comb[slot, kv, :, r * HEAD:(r + 1) * HEAD] = outs[r]
            stats = jnp.where(lanes == r, tops[r], stats)
            stats = jnp.where(lanes == HEAD // 2 + r, totals[r], stats)
        comb[slot, kv, :, QW:QW + HEAD] = stats

    def exchange_partials(slot):
        counts["remote"] = 0
        with jax.named_scope("comb_exchange"):
            wait_all([remote(comb.at[slot, kv], comb.at[slot, kv], {"kv": peer}) for peer in around])
        best = comb[slot, 0, :, QW:QW + HEAD]
        for s in range(1, 4):
            best = jnp.maximum(best, comb[slot, s, :, QW:QW + HEAD])
        best = jnp.where(lanes < HEAD // 2, best, 0.0)
        weight = [jnp.exp(jnp.where(lanes < HEAD // 2, comb[slot, s, :, QW:QW + HEAD] - best, 0.0)) for s in range(4)]
        norm = sum(pltpu.roll(comb[slot, s, :, QW:QW + HEAD], HEAD // 2, 1) * weight[s] for s in range(4))
        inverse = 1.0 / jnp.where(norm > 0, norm, 1.0)
        heads = []
        for r in range(HEADS):
            mixed = sum(comb[slot, s, :, r * HEAD:(r + 1) * HEAD] * weight[s][:, r:r + 1] for s in range(4))
            heads.append(mixed * inverse[:, r:r + 1])
        return jnp.concatenate(heads, axis=-1).astype(BF16)

    def half_sums(slot, left, w_ref, ready):
        def run(c):
            out = dot(left, w_ref[c])
            part[slot, 2 * c] = out[:, :PIECE]
            part[slot, 2 * c + 1] = out[:, PIECE:]
        copies = []
        with jax.named_scope("halves"):
            for i in range(2):
                run(2 * (1 - core) + i)
                copies.append(remote(part.at[slot, pl.ds(4 * (1 - core) + 2 * i, 2)], rs_buf.at[slot, pl.ds(2 * i, 2)], mate))
            for i in range(2):
                run(2 * core + i)
                copies[i].wait()
                for j in (2 * i, 2 * i + 1):
                    hs_buf[slot, j] = part[slot, 4 * core + j] + rs_buf[slot, j]
                ready(i)

    def reduce_plane(slot, left, w_ref, h_from, h_to, finish):
        sends = []
        half_sums(slot, left, w_ref, lambda i: sends.append(
            remote(hs_buf.at[slot, pl.ds(2 * i, 2)], y_buf.at[slot // 2, pl.ds(2 * i, 2)], across)))
        with jax.named_scope("reduce_plane"):
            backs = []
            for i in range(2):
                sends[i].wait()
                for j in (2 * i, 2 * i + 1):
                    p = 4 * core + j
                    hbuf[h_to, p] = bf(finish(hbuf[h_from, p], hs_buf[slot, j] + y_buf[slot // 2, j]))
                span = hbuf.at[h_to, pl.ds(4 * core + 2 * i, 2)]
                backs.append(remote(span, span, mate))
            wait_all(backs)

    def scatter_all(slot):
        with jax.named_scope("all_z"):
            i_z = slot // 2
            copies = [remote(hs_buf.at[slot, peer], zr_buf.at[i_z, kv], {"kv": peer}) for peer in around]
            zr_buf[i_z, kv] = hs_buf[slot, kv]
            wait_all(copies)
            gather[i_z, side, 4 * core + kv] = zr_buf[i_z, 0] + zr_buf[i_z, 1] + zr_buf[i_z, 2] + zr_buf[i_z, 3]

    def gather_all(slot, h_from, h_to, finish):
        i_z = slot // 2
        with jax.named_scope("all_gather"):
            own = gather.at[i_z, side, 4 * core + kv]
            relays = [remote(own, own, mate)]
            sends = []
            for j in (2, 1, 3):
                to = lax.rem(kv + j, 4)
                sends.append((remote(own, own, {"kv": to}), side, j))
            for j in (2, 1, 3):
                to = lax.rem(kv + j, 4)
                sends.append((remote(own, own, {"kv": to, "tp": lax.rem(tp + 2, 4)}), 1 - side, j))
            sends.insert(0, (remote(own, own, across), 1 - side, 0))
            order = sorted(range(7), key=lambda n: (sends[n][2] == 2, n))
            for n in order:
                copy, s, j = sends[n]
                copy.wait()
                got = gather.at[i_z, s, 4 * core + lax.rem(kv + 4 - j, 4)]
                relays.append(remote(got, got, mate))
            wait_all(relays)
        for p in range(8):
            hbuf[h_to, p] = bf(finish(hbuf[h_from, p], gather[i_z, 0, p] + gather[i_z, 1, p]))

    def mlp(slot, gain_row, h_slot, gu, dn, up, down):
        norm_to_u(h_slot, gain_row)
        acc = jnp.zeros((BATCH, 2 * FFW), F32)
        with jax.named_scope("gate_up"):
            wait_all(up)
            for c in range(4):
                acc = acc + dot(u_block(c), gu[c])
        gate, upper = acc[:, :FFW], acc[:, FFW:]
        act = gate * (1.0 / (1.0 + jnp.exp(-gate))) * upper
        keep = jnp.logical_or(kv < 3, lax.broadcasted_iota(jnp.int32, (BATCH, FFW), 1) >= 128)
        act = jnp.where(keep, act, 0.0).astype(BF16)
        wait_all(down)
        half_sums(slot, act, dn, lambda i: None)
        scatter_all(slot)

    def new_copies():
        return [pltpu.make_async_copy(kv_v.at[i], out, osem.at[i]) for i, out in enumerate((k_out, v_out))]

    def self_attention(wkv, ks, vs, gu):
        def copies_q(c):
            return [copy_a(wq1_h, c)] + [
                pltpu.make_async_copy(w_h.at[pl.ds(c * BLK, BLK), :], wkv.at[c, :, pl.ds(i * KVW, KVW)], wsem.at[20 + 2 * c + i])
                for i, w_h in enumerate((wk_h, wv_h))]

        for c in range(4):
            start_all(copies_q(c))

        barrier = pltpu.get_barrier_semaphore()
        peers = [{"kv": peer} for peer in around] + [{"kv": peer, "tp": lax.rem(tp + 2, 4)} for peer in around] + [mate, across]
        for peer in peers:
            pl.semaphore_signal(barrier, inc=1, device_id=peer, device_id_type=MESH)

        with jax.named_scope("first_wait"):
            wait_all(first)
        for p in range(8):
            hbuf[0, p] = x_v[:, p * PIECE:(p + 1) * PIECE].astype(F32)
        gains_v[0] = raw_v[0].astype(F32)
        norm_to_u(0, 0)
        angles = seq.astype(F32) * rope_v[0]
        cos_t, sin_t = cos_sin(angles)
        rope_v[1] = cos_t
        rope_v[2] = sin_t * jnp.where(lanes < HEAD // 2, -1.0, 1.0)
        wait_all(later)
        for i in range(1, 4):
            gains_v[i] = raw_v[i].astype(F32)

        def rope(z):
            return bf(z * rope_v[1] + pltpu.roll(z, HEAD // 2, 1) * rope_v[2])

        acc_q = jnp.zeros((BATCH, QW), F32)
        acc_kv = jnp.zeros((BATCH, 2 * KVW), F32)
        with jax.named_scope("qkv"):
            for c in range(4):
                wait_all(copies_q(c))
                if c == 1:
                    caches = [local(ks_h, ks), local(vs_h, vs)]
                elif c == 2:
                    start_all([copy_o(wo1_h, i) for i in range(4)])
                left = u_block(c)
                acc_q = acc_q + dot(left, buf_a[c])
                acc_kv = acc_kv + dot(left, wkv[c])
        query = [rope(acc_q[:, r * HEAD:(r + 1) * HEAD]) for r in range(HEADS)]
        key_new = [rope(acc_kv[:, g * HEAD:(g + 1) * HEAD]) for g in range(GROUPS)]
        val_new = [bf(acc_kv[:, KVW + g * HEAD:KVW + (g + 1) * HEAD]) for g in range(GROUPS)]
        for g in range(GROUPS):
            kv_v[0, :, g * HEAD:(g + 1) * HEAD] = key_new[g].astype(BF16)
            kv_v[1, :, g * HEAD:(g + 1) * HEAD] = val_new[g].astype(BF16)
        put_queries(query)
        wait_all(caches)
        with jax.named_scope("self_scores"):
            scores(ks, s_self)
        slot_ids = kv * SLOTS + lax.broadcasted_iota(jnp.int32, (BATCH, SLOTS), 1)
        visible = slot_ids < seq
        owner = jnp.logical_and(seq >= kv * SLOTS, seq < (kv + 1) * SLOTS)
        tops, totals, news = [], [], []
        for pair in range(HEADS // 2):
            both = []
            for r in (2 * pair, 2 * pair + 1):
                s = jnp.where(visible, s_self[r] * SCALE, MASK_VALUE)
                new = jnp.sum(query[r] * key_new[r // PER], axis=-1, keepdims=True) * SCALE
                new = jnp.where(owner, new, MASK_VALUE)
                top = jnp.maximum(jnp.max(s, axis=-1, keepdims=True), new)
                prob = jnp.where(visible, jnp.exp(s - top), 0.0)
                new_prob = jnp.where(owner, jnp.exp(new - top), 0.0)
                tops.append(top)
                totals.append(jnp.sum(prob, axis=-1, keepdims=True) + new_prob)
                news.append(new_prob)
                both.append(prob)
            p_self[2 * pair * BATCH:(2 * pair + 2) * BATCH, :] = jnp.concatenate(both, axis=0).astype(BF16)
        with jax.named_scope("self_weigh"):
            weigh(vs, p_self)
        outs = [o_v[r] + news[r] * val_new[r // PER] for r in range(HEADS)]
        with jax.named_scope("barrier"):
            pl.semaphore_wait(barrier, len(peers))
        put_partials(0, outs, tops, totals)

    def self_rest(dn, gu):
        start_all(new_copies())
        start_all(copies_up(wg1_h, wu1_h, gu))
        start_all(copies_down(wd1_h, dn))
        start_all(copies_a(wq2_h))
        attn = exchange_partials(0)
        wait_all(copies_o(wo1_h))
        reduce_plane(0, attn, buf_o, 0, 1, lambda h, s: h + s)
        start_all(copies_o(wo2_h))
        mlp(1, 1, 1, gu, dn, copies_up(wg1_h, wu1_h, gu), copies_down(wd1_h, dn))

    up_space = pltpu.VMEM((4, BLK, 2 * FFW), BF16)
    down_space = pltpu.VMEM((4, FFW, BLK), BF16)

    def phase_one(gu):
        pl.run_scoped(functools.partial(self_attention, gu=gu), pltpu.VMEM((4, BLK, 2 * KVW), BF16),
                      pltpu.VMEM((BATCH, GROUPS, SLOTS, HEAD), BF16), pltpu.VMEM((BATCH, GROUPS, SLOTS, HEAD), BF16))
        pl.run_scoped(functools.partial(self_rest, gu=gu), down_space)

    pl.run_scoped(phase_one, up_space)

    visible_tile = seen_here > 0
    row_on = jnp.where(seen > 0, 1.0, 0.0)

    def scope_two(kx, vx):
        caches = [local(kx_h, kx), local(vx_h, vx)]
        gather_all(1, 1, 2, lambda h, s: h + s)
        norm_to_u(2, 2)
        acc = jnp.zeros((BATCH, QW), F32)
        with jax.named_scope("q_cross"):
            wait_all(copies_a(wq2_h))
            for c in range(4):
                acc = acc + dot(u_block(c), buf_a[c])
        query = []
        for r in range(HEADS):
            z = acc[:, r * HEAD:(r + 1) * HEAD]
            z = z * lax.rsqrt(jnp.mean(z * z, axis=-1, keepdims=True) + NORM_EPS) * qn_v[...].astype(F32)
            query.append(bf(z))
        for r in range(HEADS):
            qc_v[r * BATCH:(r + 1) * BATCH, :] = query[r]
        with jax.named_scope("cross_scores"):
            wait_all(caches)
            q = qc_v[...].astype(BF16)
            for b in range(BATCH):
                s = lax.dot_general(q, kx[b * STEP:b * STEP + WIN, :], (((1,), (1,)), ((), ())),
                                    preferred_element_type=F32)
                for r in range(HEADS):
                    s_cross[r, b:b + 1, :] = s[r * BATCH + b:r * BATCH + b + 1, :]
        place = lax.broadcasted_iota(jnp.int32, (BATCH, WIN), 1) - 2 * lax.broadcasted_iota(jnp.int32, (BATCH, WIN), 0)
        inside = jnp.logical_and(place >= 0, place < 2 * TOK)
        tops, totals = [], []
        for pair in range(HEADS // 2):
            both = []
            for r in (2 * pair, 2 * pair + 1):
                mine = jnp.logical_and(inside, lax.rem(place + 16, 2) == r // PER)
                s = jnp.where(mine, s_cross[r] * SCALE, MASK_VALUE)
                top = jnp.max(s, axis=-1, keepdims=True)
                prob = jnp.where(mine, jnp.exp(s - top), 0.0)
                tops.append(jnp.where(visible_tile, top, MASK_VALUE))
                totals.append(jnp.where(visible_tile, jnp.sum(prob, axis=-1, keepdims=True), 0.0))
                both.append(prob)
            p_cross[2 * pair * BATCH:(2 * pair + 2) * BATCH, :] = jnp.concatenate(both, axis=0).astype(BF16)
        with jax.named_scope("cross_weigh"):
            for b in range(BATCH):
                o = dot(p_cross[...], vx[b * STEP:b * STEP + WIN, :])
                for r in range(HEADS):
                    o_v[r, b:b + 1, :] = o[r * BATCH + b:r * BATCH + b + 1, :]
        outs = [jnp.where(visible_tile, o_v[r], 0.0) for r in range(HEADS)]
        put_partials(1, outs, tops, totals)

    pl.run_scoped(scope_two, pltpu.VMEM((ROWS, HEAD), BF16), pltpu.VMEM((ROWS, HEAD), BF16))

    def gate(i):
        return jnp.tanh(jnp.full((BATCH, HEAD), gates_ref[i], F32))[:, 0:1] * row_on

    def scope_three(gu, dn):
        start_all(copies_up(wg2_h, wu2_h, gu))
        start_all(copies_down(wd2_h, dn))
        attn = exchange_partials(1)
        wait_all(copies_o(wo2_h))
        reduce_plane(2, attn, buf_o, 2, 3, lambda h, s: h + gate(0) * s)
        mlp(3, 3, 3, gu, dn, copies_up(wg2_h, wu2_h, gu), copies_down(wd2_h, dn))

    pl.run_scoped(scope_three, up_space, down_space)
    gather_all(3, 3, 4, lambda h, s: h + gate(1) * s)
    with jax.named_scope("put_h"):
        for p in range(8):
            x_v[:, p * PIECE:(p + 1) * PIECE] = hbuf[4, p].astype(BF16)
        put = pltpu.make_async_copy(x_v, h_out, osem.at[2])
        put.start()
        put.wait()
        for copy in new_copies():
            copy.wait()


def put_out(h_in, k_in, v_in, h_out, k_out, v_out):
    h_out[...] = h_in[...]
    for src, dst in ((k_in, k_out), (v_in, v_out)):
        dst[...] = src[...].astype(F32).reshape(BATCH, GROUPS, HEAD).astype(BF16)


def solution(mesh):
    rows_spec = P('dp', None)
    cache_spec = P('dp', 'tp', 'kv', None)
    new_spec = P('dp', 'tp', None)
    col_spec = P(None, 'tp')
    row_spec = P('tp', None)
    vec_spec = P(None)
    in_specs = (rows_spec, cache_spec, cache_spec, P('dp'), cache_spec, cache_spec, rows_spec,
                vec_spec, col_spec, col_spec, col_spec, row_spec, vec_spec, col_spec, col_spec, row_spec,
                vec_spec, col_spec, vec_spec, row_spec, vec_spec, vec_spec, col_spec, col_spec, row_spec)
    out_specs = (rows_spec, new_spec, new_spec)

    def device_step(x, ks_cache, vs_cache, seq_len, kx_cache, vx_cache, tile_vis, attn_norm, wq_self, wk_self, wv_self, wo_self, mlp_norm, wg_self, wu_self, wd_self, xattn_norm, wq_cross, q_norm, wo_cross, cross_gates, xmlp_norm, wg_cross, wu_cross, wd_cross):
        freqs = jnp.asarray(np.tile(rope_freqs(HEAD)[None, :], (BATCH, 1)))
        norms = [gain.reshape(HID // HEAD, HEAD) for gain in (attn_norm, mlp_norm, xattn_norm, xmlp_norm)]
        kx_rows, vx_rows = [cache.transpose(0, 2, 1, 3).reshape(ROWS, HEAD) for cache in (kx_cache, vx_cache)]
        hbm = pl.BlockSpec(memory_space=pl.ANY)
        smem = pl.BlockSpec(memory_space=pltpu.SMEM)
        vmem = pl.BlockSpec(memory_space=pltpu.VMEM)
        piece = (8, BATCH, PIECE)
        scratch = [
            pltpu.VMEM((BATCH, HID), BF16), pltpu.VMEM((2, BATCH, KVW), BF16), pltpu.VMEM((4, HID // HEAD, HEAD), BF16), pltpu.VMEM((1, HEAD), BF16),
            pltpu.VMEM((4, HID // HEAD, HEAD), F32), pltpu.VMEM((3, BATCH, HEAD), F32),
            pltpu.VMEM((4, BLK, BLK), BF16), pltpu.VMEM((4, BLK, BLK), BF16),
            pltpu.VMEM(piece, F32), pltpu.VMEM((HEADS * BATCH, 2 * HEAD), F32), pltpu.VMEM((HEADS * BATCH, HEAD), F32), pltpu.VMEM((HEADS, BATCH, HEAD), F32),
            pltpu.VMEM((HEADS, BATCH, SLOTS), F32), pltpu.VMEM((HEADS * BATCH, SLOTS), BF16),
            pltpu.VMEM((HEADS, BATCH, WIN), F32), pltpu.VMEM((HEADS * BATCH, WIN), BF16),
            pltpu.VMEM((2, 4, BATCH, QW + HEAD), F32),
            pltpu.VMEM((4,) + piece, F32), pltpu.VMEM((4, 4, BATCH, PIECE), F32),
            pltpu.VMEM((4, 4, BATCH, PIECE), F32), pltpu.VMEM((2, 4, BATCH, PIECE), F32),
            pltpu.VMEM((2, 4, BATCH, PIECE), F32), pltpu.VMEM((2, 2) + piece, F32),
            pltpu.VMEM((5,) + piece, F32),
            pltpu.SemaphoreType.DMA((N_LOCAL,)), pltpu.SemaphoreType.DMA((28,)), pltpu.SemaphoreType.DMA((3,)), pltpu.SemaphoreType.DMA((N_REMOTE,)), pltpu.SemaphoreType.DMA((N_REMOTE,)),
        ]
        h, key_new, val_new = pl.pallas_call(
            kernel,
            out_shape=(jax.ShapeDtypeStruct((BATCH, HID), BF16), jax.ShapeDtypeStruct((BATCH, KVW), BF16),
                       jax.ShapeDtypeStruct((BATCH, KVW), BF16)),
            in_specs=[hbm] * 7 + [smem] * 3 + [hbm] * 16,
            out_specs=(hbm, hbm, hbm),
            scratch_shapes=scratch,
            compiler_params=pltpu.CompilerParams(collective_id=0, has_side_effects=True, vmem_limit_bytes=VMEM_LIMIT),
        )(x, *norms, q_norm.reshape(1, HEAD), freqs, cross_gates, seq_len, tile_vis.T, ks_cache, vs_cache, kx_rows, vx_rows,
          wq_self, wk_self, wv_self, wo_self, wg_self, wu_self, wd_self, wq_cross, wo_cross, wg_cross, wu_cross, wd_cross)
        return pl.pallas_call(
            put_out,
            out_shape=(jax.ShapeDtypeStruct((BATCH, HID), BF16), jax.ShapeDtypeStruct((BATCH, GROUPS, HEAD), BF16),
                       jax.ShapeDtypeStruct((BATCH, GROUPS, HEAD), BF16)),
            in_specs=[vmem] * 3, out_specs=(vmem,) * 3)(h, key_new, val_new)

    return jax.shard_map(device_step, mesh=mesh, in_specs=in_specs, out_specs=out_specs, check_vma=False)
```

time: 105 us -> 78.5 us (0.75)
  local copies, waits for them, and re-layouts: 20.1 us -> 0 us
  Pallas kernels: 83.2 us -> 77.6 us
    unnamed x12 -> x0, local copies, waits for them, and re-layouts: 15.7 us -> none
    pallas_call x1, Pallas kernels: 83.2 us -> 76.1 us  [device_step(): pl.pallas_call(kernel, out_shape=(jax.ShapeDtypeStruct((BATCH, HID), BF16...]
    another operation x9 -> x0, local copies, waits for them, and re-layouts: 3.72 us -> none  [the longest x8 3.13 us: device_step(): jnp.stack([attn_norm, mlp_norm, xattn_norm, xmlp_norm, jnp.pad(q_norm, (0...]
    pallas_call x0 -> x1, Pallas kernels: none -> 1.54 us  [device_step(): pl.pallas_call(put_out, out_shape=(jax.ShapeDtypeStruct((BATCH, HID), BF1...]
where the time goes in v2:
time: 78.5 us; the launch traced here: 78.3 us
  Pallas kernels  77.6 us (99%)
    pallas_call x1, Pallas kernels, device_step(): pl.pallas_call(kernel, out_shape=(jax.ShapeDtypeStruct((BATCH, HID), BF16...  76.1 us

profile of v2, /device:TPU:0, one launch (start us, length us, event | category | flops | bytes accessed | tf_op | source)
XLA Modules:
  0.0 78.3 jit_solution(14626309855635951817)
XLA Ops:
  0.6 76.1 %shard_map.265 = (bf16[8,5120]{1,0:T(8,128)(2,1)}, bf16[8,256]{1,0:T(8,128)(2,1)}, bf16[8,256]{1,0:T(8,128)(2,1)}) custom-call(bf16[8,5120]{1,0:T(8,128)(2,1)} %x_h.1, bf16[40,128]{1,0:T(8,128)(2,1)} %bitcast.14, bf16[40,128]{1,0:T(8,128)(2,1)} %bitcast.15, bf16[40,128]{1,0:T(8,128)(2,1)} %bitcast.16, bf16[40,128]{1,0:T(8,128)(2,1)} %bitcast.17, ...), custom_call_target="tpu_custom_call" | custom-call | tf_op jit(solution)/shard_map/pallas_call | solution.py:510
  76.8 1.5 %shard_map.266 = (bf16[8,5120]{1,0:T(8,128)(2,1)}, bf16[8,2,128]{2,1,0:T(2,128)(2,1)}, bf16[8,2,128]{2,1,0:T(2,128)(2,1)}) custom-call(bf16[8,5120]{1,0:T(8,128)(2,1)} %get-tuple-element.6.h_in, bf16[8,256]{1,0:T(8,128)(2,1)} %get-tuple-element.7.k_in, bf16[8,256]{1,0:T(8,128)(2,1)} %get-tuple-element.8.v_in), custom_call_target="tpu_custom_call" | custom-call | tf_op jit(solution)/shard_map/pallas_call | solution.py:520

commit v3 on v2

--- a/solution.py
+++ b/solution.py
@@ -295,13 +295,15 @@
         return [pltpu.make_async_copy(kv_v.at[i], out, osem.at[i]) for i, out in enumerate((k_out, v_out))]
 
     def self_attention(wkv, ks, vs, gu):
-        def copies_q(c):
-            return [copy_a(wq1_h, c)] + [
-                pltpu.make_async_copy(w_h.at[pl.ds(c * BLK, BLK), :], wkv.at[c, :, pl.ds(i * KVW, KVW)], wsem.at[20 + 2 * c + i])
-                for i, w_h in enumerate((wk_h, wv_h))]
-
-        for c in range(4):
-            start_all(copies_q(c))
+        def copies_q(i):
+            src, c, lo = pl.ds(i * PIECE, PIECE), i // 2, (i % 2) * PIECE
+            return [pltpu.make_async_copy(wq1_h.at[src, :], buf_a.at[c, pl.ds(lo, PIECE), :], wsem.at[8 + i]),
+                    pltpu.make_async_copy(wk_h.at[src, :], wkv.at[c, pl.ds(lo, PIECE), pl.ds(0, KVW)], wsem.at[16 + i]),
+                    pltpu.make_async_copy(wv_h.at[src, :], wkv.at[c, pl.ds(lo, PIECE), pl.ds(KVW, KVW)],
+                                          wsem.at[i if i < 4 else 20 + i])]
+
+        for i in range(3):
+            start_all(copies_q(i))
 
         barrier = pltpu.get_barrier_semaphore()
         peers = [{"kv": peer} for peer in around] + [{"kv": peer, "tp": lax.rem(tp + 2, 4)} for peer in around] + [mate, across]
@@ -328,15 +330,19 @@
         acc_q = jnp.zeros((BATCH, QW), F32)
         acc_kv = jnp.zeros((BATCH, 2 * KVW), F32)
         with jax.named_scope("qkv"):
-            for c in range(4):
-                wait_all(copies_q(c))
-                if c == 1:
+            for i in range(8):
+                wait_all(copies_q(i))
+                if i < 5:
+                    start_all(copies_q(i + 3))
+                elif i == 5:
                     caches = [local(ks_h, ks), local(vs_h, vs)]
-                elif c == 2:
-                    start_all([copy_o(wo1_h, i) for i in range(4)])
-                left = u_block(c)
-                acc_q = acc_q + dot(left, buf_a[c])
-                acc_kv = acc_kv + dot(left, wkv[c])
+                    start_all([copy_o(wo1_h, n) for n in (0, 1)])
+                elif i == 6:
+                    start_all([copy_o(wo1_h, n) for n in (2, 3)])
+                left = u_v[i].astype(BF16)
+                c, span = i // 2, slice((i % 2) * PIECE, (i % 2) * PIECE + PIECE)
+                acc_q = acc_q + dot(left, buf_a[c, span, :])
+                acc_kv = acc_kv + dot(left, wkv[c, span, :])
         query = [rope(acc_q[:, r * HEAD:(r + 1) * HEAD]) for r in range(HEADS)]
         key_new = [rope(acc_kv[:, g * HEAD:(g + 1) * HEAD]) for g in range(GROUPS)]
         val_new = [bf(acc_kv[:, KVW + g * HEAD:KVW + (g + 1) * HEAD]) for g in range(GROUPS)]

time: 78.5 us -> 79.5 us (1.013)
  Pallas kernels: 77.6 us -> 78.6 us
    pallas_call x1, Pallas kernels: 76.1 us -> 77.1 us  [device_step(): pl.pallas_call(kernel, out_shape=(jax.ShapeDtypeStruct((BATCH, HID), BF16...]
where the time goes in v3:
time: 79.5 us; the launch traced here: 79.3 us
  Pallas kernels  78.6 us (99%)
    pallas_call x1, Pallas kernels, device_step(): pl.pallas_call(kernel, out_shape=(jax.ShapeDtypeStruct((BATCH, HID), BF16...  77.1 us

profile of v3, /device:TPU:0, one launch (start us, length us, event | category | flops | bytes accessed | tf_op | source)
XLA Modules:
  0.0 79.3 jit_solution(14877181533115546672)
XLA Ops:
  0.6 77.1 %shard_map.265 = (bf16[8,5120]{1,0:T(8,128)(2,1)}, bf16[8,256]{1,0:T(8,128)(2,1)}, bf16[8,256]{1,0:T(8,128)(2,1)}) custom-call(bf16[8,5120]{1,0:T(8,128)(2,1)} %x_h.1, bf16[40,128]{1,0:T(8,128)(2,1)} %bitcast.14, bf16[40,128]{1,0:T(8,128)(2,1)} %bitcast.15, bf16[40,128]{1,0:T(8,128)(2,1)} %bitcast.16, bf16[40,128]{1,0:T(8,128)(2,1)} %bitcast.17, ...), custom_call_target="tpu_custom_call" | custom-call | tf_op jit(solution)/shard_map/pallas_call | solution.py:516
  77.8 1.5 %shard_map.266 = (bf16[8,5120]{1,0:T(8,128)(2,1)}, bf16[8,2,128]{2,1,0:T(2,128)(2,1)}, bf16[8,2,128]{2,1,0:T(2,128)(2,1)}) custom-call(bf16[8,5120]{1,0:T(8,128)(2,1)} %get-tuple-element.6.h_in, bf16[8,256]{1,0:T(8,128)(2,1)} %get-tuple-element.7.k_in, bf16[8,256]{1,0:T(8,128)(2,1)} %get-tuple-element.8.v_in), custom_call_target="tpu_custom_call" | custom-call | tf_op jit(solution)/shard_map/pallas_call | solution.py:526
